TPU v7x, 128 devices: a whole 4x4x4 slice. The times are simulated.
128 devices in a mesh: dom: 128 (over y, z, x, core).
Axes of the slice: x: 4, y: 4, z: 4, core: 2. Of those that a mesh axis runs over, the one named last changes fastest.
Arguments:
- features: bfloat16 [65536, 512], P('dom'), may hold values from -6 to 6
- weights: bfloat16 [3, 512, 512], replicated, may hold values from -0.078125 to 0.078125
- halo_send: int32 [128, 128, 4], P('dom'), may hold values from 0 to 511
- nbr_index: int32 [65536, 2, 8], P('dom'), may hold values from 0 to 1023
- tile_count: int32 [128], P('dom'), may hold values from 1 to 16, as said below
- edge_ends: int32 [2048, 2, 256], P('dom'), may hold values from 0 to 511
- neg_ids: int32 [1024], P('dom'), may hold values from 0 to 511
Outputs:
- weight_grad: float32 [3, 512, 512], replicated
- mean_loss: float32 [], replicated
- pre_grad: bfloat16 [65536, 512], P('dom')
Inputs may be any that keep to these rules, and one draw needn't show every extreme that they name: `nbr_index`: an entry below 512 names a row of the node's own partition; an entry 512 + q * 4 + k names slot k of the halo from partition q. `tile_count`: partition 128 - 1 holds 16 tiles; every other partition holds at most 8. `edge_ends`: tile slots at or past a partition's tile_count hold no edges. `neg_ids`: entry j names a row of partition j // 8.
All inputs are finite; a program needn't handle non-finite values.
Results may differ from a plain program's by a relative error of at most 0.0012.
The roundings to bfloat16 on the way count: a program that leaves them out, or rounds other values in their place, can miss the bound.
Values may be sent and summed in bfloat16 or wider, within the bound.
A program may use at most 64 MiB of HBM per device.

v0:
```python
import jax
import jax.numpy as jnp
from jax import lax
from jax.sharding import Mesh
from jax.sharding import PartitionSpec as P

DOM = ("dom_0", "dom_1", "dom_2", "dom_3")


def sent_to_all(x, axis):
    copies = jnp.broadcast_to(x, (lax.axis_size(axis), *x.shape))
    return lax.all_to_all(copies, axis, split_axis=0, concat_axis=0, tiled=True)


def joined_along(tiles, dim):
    dims = list(tiles.shape[1:])
    dims[dim] *= tiles.shape[0]
    return jnp.moveaxis(tiles, 0, dim).reshape(dims)


def gather_axes(x, axes, dim):
    far, near = axes
    tiles = sent_to_all(sent_to_all(x, far), near)
    return joined_along(tiles.swapaxes(0, 1).reshape(-1, *x.shape), dim)


def swapped(x, axis, bit):
    return lax.ppermute(x, axis, [(i, i ^ 1 << bit) for i in range(lax.axis_size(axis))])


def split_up(x, dim, devices):
    dims = x.shape
    tiles = x.reshape(*dims[:dim], devices, dims[dim] // devices, *dims[dim + 1 :])
    return jnp.moveaxis(tiles, dim, 0)


def sum_at_owner(x, axis, dim):
    tiles = split_up(x, dim, lax.axis_size(axis))
    arrived = lax.all_to_all(tiles, axis, split_axis=0, concat_axis=0, tiled=True)
    return arrived.sum(axis=0)


def sum_by_axis(x, axes, dim):
    far, near = axes
    own = sum_at_owner(split_up(x, dim, lax.axis_size(far)), near, dim + 1)
    return jnp.sum(lax.all_to_all(own, far, 0, 0, tiled=True), axis=0)


def filled_up(lines, devices):
    spare = -len(lines) % devices
    return jnp.pad(lines, [(0, spare)] + [(0, 0)] * (lines.ndim - 1))


def total_of(x, axes):
    own = sum_by_axis(filled_up(x, lax.axis_size(axes[0]) * lax.axis_size(axes[1])), axes, 0)
    whole = gather_axes(own, axes, 0)
    return whole[: len(x)].reshape(x.shape)


def together(arrays, axis):
    vector, at, finished = (jnp.concatenate([a.reshape(-1) for a in arrays]), 0, [])
    so_far = total_of(vector, axis)
    for a in arrays:
        finished.append(so_far[at : at + a.size].reshape(a.shape))
        at += a.size
    return tuple(finished)


def neighbour_mean(lookup, neighbours):
    running_sum = jnp.zeros((neighbours.shape[0], lookup.shape[1]), jnp.float32)
    for column in range(neighbours.shape[1]):
        running_sum = running_sum + lookup[neighbours[:, column]].astype(jnp.float32)
    return (running_sum / neighbours.shape[1]).astype(jnp.bfloat16)


def score_tile(source, target, negatives):
    source_wide = source.astype(jnp.float32)
    target_wide = target.astype(jnp.float32)
    positive = jnp.sum(source_wide * target_wide, axis=1)
    negative = lax.dot_general(
        source, negatives, (((1,), (1,)), ((), ())), preferred_element_type=jnp.float32
    )
    count_neg = negatives.shape[0]
    tile_loss = (
        jnp.sum(jnp.logaddexp(0.0, -positive)) + jnp.sum(jnp.logaddexp(0.0, negative)) / count_neg
    )
    grad_positive = -jax.nn.sigmoid(-positive)
    grad_negative = (jax.nn.sigmoid(negative) / count_neg).astype(jnp.bfloat16)
    source_grad = grad_positive[:, None] * target_wide + jnp.dot(
        grad_negative, negatives, preferred_element_type=jnp.float32
    )
    target_grad = grad_positive[:, None] * source_wide
    negative_grad = lax.dot_general(
        grad_negative, source, (((0,), (0,)), ((), ())), preferred_element_type=jnp.float32
    )
    return (tile_loss, source_grad, target_grad, negative_grad)


def on_device(features, weights, halo_send, nbr_index, tile_count, edge_ends, neg_ids):
    feature_width = features.shape[1]
    relation_count = nbr_index.shape[1]
    outgoing = features[halo_send[0]]
    incoming = lax.all_to_all(outgoing, DOM, split_axis=0, concat_axis=0, tiled=True)
    preact = jnp.dot(features, weights[0], preferred_element_type=jnp.float32)
    lookup = jnp.concatenate([features, incoming.reshape(-1, feature_width)], 0)
    means = []
    for relation in range(relation_count):
        mean_rows = neighbour_mean(lookup, nbr_index[:, relation, :])
        means.append(mean_rows)
        preact = preact + jnp.dot(
            mean_rows, weights[relation + 1], preferred_element_type=jnp.float32
        )
    embedding = preact.astype(jnp.bfloat16)
    negatives = gather_axes(embedding[neg_ids], (("dom_0", "dom_1", "dom_2"), "dom_3"), 0)
    my_tiles = tile_count[0]

    def score_local(tile_index, running):
        loss_sum, node_grad, neg_grad = running
        pair_ends = lax.dynamic_index_in_dim(edge_ends, tile_index, 0, keepdims=False)
        tile_loss, source_grad, target_grad, negative_grad = score_tile(
            embedding[pair_ends[0]], embedding[pair_ends[1]], negatives
        )
        node_grad = node_grad.at[pair_ends[0]].add(source_grad).at[pair_ends[1]].add(target_grad)
        return (loss_sum + tile_loss, node_grad, neg_grad + negative_grad)

    initial = (
        jnp.zeros((), jnp.float32),
        jnp.zeros(features.shape, jnp.float32),
        jnp.zeros(negatives.shape, jnp.float32),
    )
    far_bit = lax.axis_size(DOM).bit_length() - 2
    partner_embed, partner_ends, partner_count = swapped(
        (embedding, edge_ends, tile_count), DOM, far_bit
    )
    partner_tiles = partner_count[0]
    moved_out = jnp.maximum(my_tiles - partner_tiles, 0) // 2
    moved_in = jnp.maximum(partner_tiles - my_tiles, 0) // 2
    loss_sum, node_grad, neg_grad = lax.fori_loop(0, my_tiles - moved_out, score_local, initial)
    first_moved = partner_tiles - moved_in

    def score_table(tile_index, running):
        moved_loss, moved_neg, table = running
        pair_ends = lax.dynamic_index_in_dim(
            partner_ends, first_moved + tile_index, 0, keepdims=False
        )
        tile_loss, source_grad, target_grad, negative_grad = score_tile(
            partner_embed[pair_ends[0]], partner_embed[pair_ends[1]], negatives
        )
        table = table.at[pair_ends[0]].add(source_grad).at[pair_ends[1]].add(target_grad)
        return (moved_loss + tile_loss, moved_neg + negative_grad, table)

    empty_table = jnp.zeros(features.shape, jnp.float32)
    loss_sum, neg_grad, table = lax.fori_loop(
        0, moved_in, score_table, (loss_sum, neg_grad, empty_table)
    )
    node_grad = node_grad + swapped(table, DOM, far_bit)
    own_neg_grad = sum_by_axis(neg_grad, (("dom_0", "dom_1", "dom_2"), "dom_3"), 0)
    node_grad = node_grad.at[neg_ids].add(own_neg_grad)
    pre_grad = node_grad.astype(jnp.bfloat16)
    terms = [
        lax.dot_general(
            features, pre_grad, (((0,), (0,)), ((), ())), preferred_element_type=jnp.float32
        )
    ]
    for relation in range(relation_count):
        terms.append(
            lax.dot_general(
                means[relation],
                pre_grad,
                (((0,), (0,)), ((), ())),
                preferred_element_type=jnp.float32,
            )
        )
    weight_partial = jnp.stack(terms)
    edge_count = my_tiles.astype(jnp.float32) * edge_ends.shape[2]
    weight_sum, total_loss, edge_total = together(
        (weight_partial, loss_sum, edge_count), (("dom_0", "dom_1", "dom_2"), "dom_3")
    )
    return (weight_sum / edge_total, total_loss / edge_total, pre_grad)


def solution(mesh):
    torus = Mesh(mesh.devices.reshape(4, 4, 4, 2), ("dom_0", "dom_1", "dom_2", "dom_3"))
    in_specs = (
        P(DOM, None),
        P(),
        P(DOM, None, None),
        P(DOM, None, None),
        P(DOM),
        P(DOM, None, None),
        P(DOM),
    )
    out_specs = (P(), P(), P(DOM, None))
    return jax.shard_map(
        on_device, mesh=torus, in_specs=in_specs, out_specs=out_specs, check_vma=False
    )
```

profile of v0, /device:TPU:1, one launch (start us, length us, event | category | flops | bytes accessed | tf_op | source)
XLA Modules:
  0.0 497.1 jit_solution(15353902469451114779)
XLA Ops:
  2.2 3.1 gather_fusion.4
  6.3 11.5 %all-to-all-start = ((bf16[128,4,512]{2,1,0:T(4,128)(2,1)}), bf16[128,4,512]{2,1,0:T(4,128)(2,1)S(1)}, u32[]{:S(2)}, u32[]{:S(2)}) async-start(bf16[128,4,512]{2,1,0:T(4,128)(2,1)} %reshape.232), calls=%async_computation | async-start | bytes 1048576 | tf_op jit(solution)/shard_map/all_to_all | solution.py:103
  19.5 11.9 %all-to-all-done = bf16[128,4,512]{2,1,0:T(4,128)(2,1)S(1)} async-done(((bf16[128,4,512]{2,1,0:T(4,128)(2,1)}), bf16[128,4,512]{2,1,0:T(4,128)(2,1)S(1)}, u32[]{:S(2)}, u32[]{:S(2)}) %all-to-all-start) | async-done | bytes 524320 | tf_op jit(solution)/shard_map/all_to_all | solution.py:103
  72.0 14.3 %gather_fusion.20 = bf16[512,512]{1,0:T(8,128)(2,1)} fusion(bf16[1024,512]{1,0:T(8,128)(2,1)S(1)} %constant_dynamic-update-slice_fusion, s32[1024]{0:T(1024)S(1)} %get-tuple-element.172), kind=kCustom, calls=%fused_computation.20 | custom fusion | bytes 1050624 | tf_op jit(solution)/shard_map/gather | solution.py:72
  86.2 2.7 multiply_convert_fusion.7
  96.6 4.6 all-to-all-start.1
  107.6 3.0 collective-permute-start.2
  113.2 6.8 %all_to_all.53 = bf16[2,64,8,512]{3,2,1,0:T(8,128)(2,1)S(1)} all-to-all(bf16[2,64,8,512]{3,2,1,0:T(8,128)(2,1)S(1)} %broadcast_in_dim.15), channel_id=1, replica_groups=mesh['dom_0'=4,'dom_1'=4,'dom_2'=4,'dom_3'=2] {'dom_3'}, dimensions={0} | all-to-all | bytes 2097152 | tf_op jit(solution)/shard_map/all_to_all | solution.py:12
  122.9 20.2 %while.28 = (s32[]{:T(128)}, f32[]{:T(128)}, f32[512,512]{1,0:T(8,128)S(1)}, f32[1024,512]{1,0:T(8,128)}, s32[]{:T(128)}, /*index=5*/s32[16,2,256]{2,1,0:T(2,128...) while((s32[]{:T(128)}, f32[]{:T(128)}, ...), condition=%wide.region_6.7_spmd, body=%wide.region_0.6_spmd.sunk | while | flops 811997440 | bytes 23615768 | solution.py:138
  129.2 2.7 select_reduce_fusion.4
  139.3 3.8 convolution_add_fusion.11
  143.2 20.0 %while.29 = (s32[]{:T(128)}, f32[]{:T(128)}, f32[1024,512]{1,0:T(8,128)}, f32[512,512]{1,0:T(8,128)S(1)}, s32[]{:T(128)}, /*index=5*/s32[]{:T(128)}, s32[16,2,25...) while((s32[]{:T(128)}, f32[]{:T(128)}, ...), condition=%wide.region_13.14_spmd, body=%wide.region_7.13_spmd.sunk | while | flops 811997440 | bytes 24664392 | solution.py:153
  148.0 2.8 select_reduce_fusion.5
  152.1 3.0 scatter_fusion.1
  159.0 3.8 convolution_add_fusion.12
  165.8 6.6 %all_to_all.54 = f32[2,64,8,512]{3,2,1,0:T(8,128)} all-to-all(f32[2,64,8,512]{3,2,1,0:T(8,128)S(1)} %copy.31), channel_id=1, replica_groups=mesh['dom_0'=4,'dom_1'=4,'dom_2'=4,'dom_3'=2] {'dom_3'}, dimensions={0} | all-to-all | bytes 4194304 | tf_op jit(solution)/shard_map/all_to_all | solution.py:39
  172.3 2.9 reduce_sum.90
  175.2 148.2 %all-to-all-start.4 = ((f32[64,8,512]{2,1,0:T(8,128)}), f32[64,8,512]{2,1,0:T(8,128)}, u32[]{:S(2)}, u32[]{:S(2)}) async-start(f32[64,8,512]{2,1,0:T(8,128)} %reduce_sum.90), calls=%async_computation.4 | async-start | bytes 2097152 | tf_op jit(solution)/shard_map/all_to_all | solution.py:46
  323.4 18.0 %all-to-all-done.4 = f32[64,8,512]{2,1,0:T(8,128)} async-done(((f32[64,8,512]{2,1,0:T(8,128)}), f32[64,8,512]{2,1,0:T(8,128)}, u32[]{:S(2)}, u32[]{:S(2)}) %all-to-all-start.4) | async-done | bytes 1048608 | tf_op jit(solution)/shard_map/all_to_all | solution.py:46
  348.8 3.5 copy.34
  352.3 4.4 copy.40
  356.7 25.6 %concatenate.7 = f32[786434]{0:T(1024)} concatenate(f32[786432]{0:T(1024)} %bitcast.131, f32[1]{0:T(128)} %bitcast.41, f32[1]{0:T(128)} %bitcast.42), dimensions={0} | concatenate | bytes 6291472 | tf_op jit(solution)/shard_map/concatenate | solution.py:61
  382.3 3.8 pad.4
  386.1 6.7 %reshape_reshape.14 = f32[64,2,6145]{2,1,0:T(2,128)} reshape(f32[786560]{0:T(1024)} %pad.4) | data formatting | bytes 6292480 | tf_op jit(solution)/shard_map/reshape;reshape | solution.py:33
  394.9 8.7 %all_to_all.55 = f32[2,64,6145]{2,1,0:T(8,128)} all-to-all(f32[2,64,6145]{2,1,0:T(8,128)S(1)} %copy.35), channel_id=1, replica_groups=mesh['dom_0'=4,'dom_1'=4,'dom_2'=4,'dom_3'=2] {'dom_3'}, dimensions={0} | all-to-all | bytes 6292480 | tf_op jit(solution)/shard_map/all_to_all | solution.py:39
  407.0 28.3 %all_to_all.58 = f32[64,1,6145]{2,1,0:T(1,128)S(1)} all-to-all(f32[64,1,6145]{2,1,0:T(1,128)S(1)} %all_to_all.39), channel_id=1, replica_groups=mesh['dom_0'=4,'dom_1'=4,'dom_2'=4,'dom_3'=2] {'dom_0','dom_1','dom_2'}, dimensions={0} | all-to-all | bytes 3146240 | tf_op jit(solution)/shard_map/all_to_all | solution.py:46
  437.0 27.4 %all_to_all.56 = f32[64,1,6145]{2,1,0:T(1,128)S(1)} all-to-all(f32[64,1,6145]{2,1,0:T(1,128)S(1)} %broadcast_in_dim.16), channel_id=1, replica_groups=mesh['dom_0'=4,'dom_1'=4,'dom_2'=4,'dom_3'=2] {'dom_0','dom_1','dom_2'}, dimensions={0} | all-to-all | bytes 3146240 | tf_op jit(solution)/shard_map/all_to_all | solution.py:12
  464.8 9.0 %all_to_all.57 = f32[2,64,6145]{2,1,0:T(8,128)S(1)} all-to-all(f32[2,64,6145]{2,1,0:T(8,128)S(1)} %broadcast_in_dim.17), channel_id=1, replica_groups=mesh['dom_0'=4,'dom_1'=4,'dom_2'=4,'dom_3'=2] {'dom_3'}, dimensions={0} | all-to-all | bytes 6292480 | tf_op jit(solution)/shard_map/all_to_all | solution.py:12
  473.8 4.1 copy.36
  477.9 6.2 %reshape_reshape.15 = f32[786560]{0:T(1024)} reshape(f32[64,2,6145]{2,1,0:T(2,128)} %copy.36) | data formatting | bytes 6292480 | tf_op jit(solution)/shard_map/reshape;reshape | solution.py:18
  485.5 4.4 slice_divide_fusion
  491.2 4.6 div.63
  (132 shorter events, 101.4 us)
Async XLA Ops:
  5.3 12.4 %copy-start.18 = (s32[512,2,8]{0,2,1:T(8,128)S(1)}, s32[512,2,8]{0,2,1:T(8,128)}, u32[]{:S(2)}) copy-start(s32[512,2,8]{0,2,1:T(8,128)} %param.14) | copy-start | bytes 98308
  5.3 12.6 %copy-start = (bf16[512,512]{1,0:T(8,128)(2,1)S(1)}, bf16[512,512]{1,0:T(8,128)(2,1)}, u32[]{:S(2)}) copy-start(bf16[512,512]{1,0:T(8,128)(2,1)} %param.11) | copy-start | bytes 1572868
  6.3 25.1 %all-to-all-start = ((bf16[128,4,512]{2,1,0:T(4,128)(2,1)}), bf16[128,4,512]{2,1,0:T(4,128)(2,1)S(1)}, u32[]{:S(2)}, u32[]{:S(2)}) async-start(bf16[128,4,512]{2,1,0:T(4,128)(2,1)} %reshape.232), calls=%async_computation | async-start | bytes 1048576 | tf_op jit(solution)/shard_map/all_to_all | solution.py:103
  86.2 3.5 copy-start.15
  86.2 4.0 copy-start.13
  86.2 4.0 copy-start.14
  88.9 0.8 copy-start.5
  89.7 1.0 copy-start.7
  89.7 1.2 copy-start.8
  89.7 1.4 copy-start.9
  89.7 1.5 copy-start.10
  89.7 1.7 copy-start.11
  89.7 1.8 copy-start.12
  92.1 0.8 copy-start.3
  96.6 16.5 %all-to-all-start.1 = ((bf16[64,8,512]{2,1,0:T(8,128)(2,1)}), bf16[64,8,512]{2,1,0:T(8,128)(2,1)S(1)}, u32[]{:S(2)}, u32[]{:S(2)}) async-start(bf16[64,8,512]{2,1,0:T(8,128)(2,1)} %broadcast_in_dim.14), calls=%async_computation.1 | async-start | bytes 1048576 | tf_op jit(solution)/shard_map/all_to_all | solution.py:12
  101.3 4.2 collective-permute-start
  104.0 39.1 %collective-permute-start.1 = (s32[16,2,256]{2,1,0:T(2,128)}, s32[16,2,256]{2,1,0:T(2,128)S(1)}, u32[]{:S(2)}, u32[]{:S(2)}) collective-permute-start(s32[16,2,256]{2,1,0:T(2,128)} %param.16), channel_id=1, source_target_pairs={{0,64},{1,65},{2,66},{3,67},{4,68},{5,69},{6,70},{7,71},{8,72},{9,... | collective-permute-start | bytes 98312 | tf_op jit(solution)/shard_map/ppermute | solution.py:28
  107.6 35.5 %collective-permute-start.2 = (bf16[512,512]{1,0:T(8,128)(2,1)}, bf16[512,512]{1,0:T(8,128)(2,1)S(1)}, u32[]{:S(2)}, u32[]{:S(2)}) collective-permute-start(bf16[512,512]{1,0:T(8,128)(2,1)} %fusion.8), channel_id=1, source_target_pairs={{0,64},{1,65},{2,66},{3,67},{4,68},{5,69},{6,70},{7,71},{8,72},{9,... | collective-permute-start | bytes 1572872 | tf_op jit(solution)/shard_map/ppermute | solution.py:28
  128.5 3.4 copy-start.16
  131.9 1.0 copy-start.19
  147.4 3.5 copy-start.1
  147.4 3.5 copy-start.17
  150.8 1.3 copy-start.20
  163.2 179.5 %collective-permute-start.3 = (f32[512,512]{1,0:T(8,128)S(1)}, f32[512,512]{1,0:T(8,128)}, u32[]{:S(2)}, u32[]{:S(2)}) collective-permute-start(f32[512,512]{1,0:T(8,128)S(1)} %get-tuple-element.101), channel_id=1, source_target_pairs={{0,64},{1,65},{2,66},{3,67},{4,68},{5,69},{6,70},{7,71},{8,72},{9,... | collective-permute-start | bytes 3145736 | tf_op jit(solution)/shard_map/ppermute | solution.py:28
  175.2 166.2 %all-to-all-start.4 = ((f32[64,8,512]{2,1,0:T(8,128)}), f32[64,8,512]{2,1,0:T(8,128)}, u32[]{:S(2)}, u32[]{:S(2)}) async-start(f32[64,8,512]{2,1,0:T(8,128)} %reduce_sum.90), calls=%async_computation.4 | async-start | bytes 2097152 | tf_op jit(solution)/shard_map/all_to_all | solution.py:46
  342.7 2.6 copy-start.6
  344.2 1.7 copy-start.4
  345.4 1.0 copy-start.2
where the time goes:
time: 505 us; the launch traced here: 497 us
  starting transfers between devices  171 us (34%)
  local copies, waits for them, and re-layouts  142 us (28%)
  blocking collectives  86.8 us (17%)
  other arithmetic  35.1 us (7%)
  waiting for transfers between devices  33 us (7%)
  matrix products  19.4 us (4%)
  between operations  6.44 us (1%)
    all_to_all x1, starting transfers between devices, sum_by_axis(): return jnp.sum(lax.all_to_all(own, far, 0, 0, tiled=True), axis=0)  148 us
    gather x16, local copies, waits for them, and re-layouts, neighbour_mean(): lookup[neighbours[:, column]].astype(jnp.float32)  52.8 us
    all_to_all x3, blocking collectives, sent_to_all(): return lax.all_to_all(copies, axis, split_axis=0, concat_axis=0, tiled=True)  43.3 us
    all_to_all x1, blocking collectives, sum_by_axis(): return jnp.sum(lax.all_to_all(own, far, 0, 0, tiled=True), axis=0)  28.3 us
    concatenate x1, local copies, waits for them, and re-layouts, together(): jnp.concatenate([a.reshape(-1) for a in arrays])  25.6 us
    all_to_all x1, waiting for transfers between devices, sum_by_axis(): return jnp.sum(lax.all_to_all(own, far, 0, 0, tiled=True), axis=0)  18 us
    all_to_all x2, blocking collectives, sum_at_owner(): lax.all_to_all(tiles, axis, split_axis=0, concat_axis=0, tiled=True)  15.2 us
    all_to_all x1, waiting for transfers between devices, on_device(): lax.all_to_all(outgoing, DOM, split_axis=0, concat_axis=0, tiled=True)  11.9 us
  transfers between devices with their start and end apart: 7, of which 4 were waited for; matrix products, arithmetic and copies ran while one was open for 6% of the time, Pallas kernels for 0%

commit v1 on v0

v1 whole, which is shorter than its diff:
```python
import jax
import jax.numpy as jnp
from jax import lax
from jax.experimental import pallas as pl
from jax.experimental.pallas import tpu as pltpu
from jax.sharding import PartitionSpec as P

MESH = pl.DeviceIdType.MESH
F32 = jnp.float32
BF16 = jnp.bfloat16
STRIDES = (32, 8, 2)


def nn(a, b):
    return lax.dot_general(a, b, (((1,), (0,)), ((), ())), preferred_element_type=F32)


def nt(a, b):
    return lax.dot_general(a, b, (((1,), (1,)), ((), ())), preferred_element_type=F32)


def tn(a, b):
    return lax.dot_general(a, b, (((0,), (0,)), ((), ())), preferred_element_type=F32)


def split(x):
    hi = x.astype(BF16)
    lo = (x - hi.astype(F32)).astype(BF16)
    return hi, lo


def flat(block):
    wide = block.astype(F32)
    return wide.reshape(-1, wide.shape[-1]).astype(BF16)


def kernel(
    count_ref,
    ids_ref,
    feat_ref,
    wts_ref,
    halo_ref,
    nbr_ref,
    ends_ref,
    wout_ref,
    stat_ref,
    pre_ref,
    out_buf,
    in_buf,
    sel_ref,
    mean_ref,
    emb_ref,
    one_a,
    one_b,
    pair_ref,
    sym_ref,
    dotp_ref,
    hi_ref,
    lo_ref,
    neg_blk,
    neg_buf,
    score_ref,
    gneg_ref,
    grad_ref,
    wide_ref,
    sib_out,
    sib_in,
    rs_out,
    rs_in,
    part_ref,
    wsib_ref,
    s1_ref,
    s2_ref,
    s3_ref,
    a1_ref,
    a2_ref,
    a3_ref,
    t_out,
    t_in,
    ex_send,
    ex_recv,
    sib_send,
    sib_recv,
    w_send,
    w_recv,
    t_send,
    t_recv,
):
    me = lax.axis_index("dom")
    chip, core = me // 2, me % 2
    other = 1 - core
    sibling = me + 1 - 2 * core
    coords = (chip // 16, (chip // 4) % 4, chip % 4)
    barrier = pltpu.get_barrier_semaphore()

    def hello(s, carry):
        pl.semaphore_signal(
            barrier, inc=1, device_id=((me + s) % 128,), device_id_type=MESH
        )
        return carry

    lax.fori_loop(1, 128, hello, 0)

    def remote(src, dst, send, recv, to):
        return pltpu.make_async_remote_copy(
            src_ref=src,
            dst_ref=dst,
            send_sem=send,
            recv_sem=recv,
            device_id=(to,),
            device_id_type=MESH,
        )

    def spread(src_of, dst, phase):
        def body(s, carry):
            to = (chip + s) % 64
            remote(
                src_of(to), dst, ex_send.at[phase], ex_recv.at[phase], 2 * to + core
            ).start()
            return carry

        lax.fori_loop(1, 64, body, 0)

    def arrived(buf, phase):
        whole = buf.at[pl.ds(0, 63)]
        remote(whole, whole, ex_send.at[phase], ex_recv.at[phase], sibling).wait_recv()

    def left(buf, phase):
        whole = buf.at[pl.ds(0, 63)]
        remote(whole, whole, ex_send.at[phase], ex_recv.at[phase], sibling).wait_send()

    halo_ids = halo_ref[...]
    pick = jnp.where(
        lax.broadcasted_iota(jnp.int32, (512, 512), 0) == halo_ids, 1.0, 0.0
    ).astype(BF16)
    out_buf[...] = tn(pick, feat_ref[...]).reshape(64, 8, 512).astype(BF16)
    in_buf[core, chip] = out_buf[chip]

    pl.semaphore_wait(barrier, 127)
    spread(lambda to: out_buf.at[to], in_buf.at[core, chip], 0)

    count = count_ref[0]
    live = lax.broadcasted_iota(jnp.int32, (16, 256), 0) < count
    pair_ref[...] = jnp.zeros_like(pair_ref)

    def add_tiles(group, carry):
        for t in range(4):
            tile = group * 4 + t
            row = ends_ref[pl.ds(tile, 1), :]
            used = lax.broadcasted_iota(jnp.int32, (1, 256), 0) + tile < count
            source = jnp.where(used, row[:, :256], -1)
            target = row[:, 256:]
            for h in range(4):
                nodes = lax.broadcasted_iota(jnp.int32, (128, 256), 0) + h * 128
                at = (slice(h * 128, h * 128 + 128), slice(t * 256, t * 256 + 256))
                one_a[at] = jnp.where(nodes == source, 1.0, 0.0).astype(BF16)
                one_b[at] = jnp.where(nodes == target, 1.0, 0.0).astype(BF16)
        pair_ref[...] += nt(one_a[...], one_b[...])
        return carry

    lax.fori_loop(0, 4, add_tiles, 0)
    sym_ref[...] = pair_ref[...] + pair_ref[...].T

    def count_rows(step, carry):
        rows = pl.ds(pl.multiple_of(step * 32, 32), 32)
        ids = nbr_ref[rows, :]
        past = ids - 512
        slot = (
            512
            + ((past // 4) % 2) * 512
            + (past // 8) * 8
            + core * 4
            + past % 4
        )
        ids = jnp.where(ids < 512, ids, slot)
        for r in range(2):
            for part in range(3):
                lanes = lax.broadcasted_iota(jnp.int32, (32, 512), 1) + part * 512
                total = jnp.zeros((32, 512), F32)
                for j in range(8):
                    col = ids[:, r * 8 + j : r * 8 + j + 1]
                    total = total + jnp.where(lanes == col, 1.0, 0.0)
                sel_ref[r, rows, part * 512 : part * 512 + 512] = total.astype(BF16)
        return carry

    lax.fori_loop(0, 16, count_rows, 0)

    arrived(in_buf.at[core], 0)
    to_sib = remote(
        in_buf.at[core], in_buf.at[core], sib_send.at[0], sib_recv.at[0], sibling
    )
    to_sib.start()
    preact = nn(feat_ref[...], wts_ref[0])
    to_sib.wait()
    left(out_buf, 0)

    table = flat(in_buf[...].reshape(1024, 512))
    for r in range(2):
        total = nn(sel_ref[r, :, :512], feat_ref[...]) + nn(sel_ref[r, :, 512:], table)
        mean = (total * 0.125).astype(BF16)
        mean_ref[r] = mean
        preact = preact + nn(mean, wts_ref[r + 1])
    emb_ref[...] = preact.astype(BF16)

    row_of = lax.broadcasted_iota(jnp.int32, (8, 512), 0)
    named = jnp.zeros((8, 512), jnp.int32)
    for j in range(8):
        named = jnp.where(row_of == j, ids_ref[j], named)
    pick_neg = jnp.where(
        named == lax.broadcasted_iota(jnp.int32, (8, 512), 1), 1.0, 0.0
    ).astype(BF16)
    own_neg = nn(pick_neg, emb_ref[...]).astype(BF16)
    neg_blk[...] = own_neg
    neg_buf[core, chip] = own_neg
    spread(lambda to: neg_blk, neg_buf.at[core, chip], 1)

    dotp_ref[...] = nt(emb_ref[...], emb_ref[...])

    def positive_rows(step, loss):
        rows = pl.ds(pl.multiple_of(step * 32, 32), 32)
        dots, weight = dotp_ref[rows, :], sym_ref[rows, :]
        small = jnp.exp(-jnp.abs(dots))
        below = jnp.where(dots >= 0, small, 1.0) / (1.0 + small)
        loss = loss + weight * (jnp.maximum(-dots, 0.0) + jnp.log1p(small))
        hi, lo = split(-weight * below)
        hi_ref[rows, :] = hi
        lo_ref[rows, :] = lo
        return loss

    loss_pos = lax.fori_loop(0, 16, positive_rows, jnp.zeros((32, 512), F32))
    emb = emb_ref[...]
    grad_ref[...] = nn(hi_ref[...], emb) + nn(lo_ref[...], emb)
    degree = jnp.sum(pair_ref[...], axis=1, keepdims=True)
    hi, lo = split(emb.astype(F32) * degree)
    hi_ref[...] = hi
    lo_ref[...] = lo

    arrived(neg_buf.at[core], 1)
    to_sib = remote(
        neg_buf.at[core], neg_buf.at[core], sib_send.at[1], sib_recv.at[1], sibling
    )
    to_sib.start()
    to_sib.wait()
    whole = neg_buf.at[core].at[pl.ds(0, 63)]
    remote(whole, whole, ex_send.at[1], ex_recv.at[1], sibling).wait_send()

    negs = flat(neg_buf[...].reshape(1024, 512))
    score_ref[...] = nt(emb_ref[...], negs)

    def negative_rows(step, loss):
        rows = pl.ds(pl.multiple_of(step * 16, 16), 16)
        dots = score_ref[rows, :]
        small = jnp.exp(-jnp.abs(dots))
        above = jnp.where(dots >= 0, 1.0, small) / (1.0 + small)
        gneg_ref[rows, :] = (above * (1.0 / 1024)).astype(BF16)
        soft = jnp.maximum(dots, 0.0) + jnp.log1p(small)
        many = jnp.sum(pair_ref[rows, :], axis=1, keepdims=True)
        return loss + soft * many

    loss_neg = lax.fori_loop(0, 32, negative_rows, jnp.zeros((16, 1024), F32))
    wide = tn(gneg_ref[...], hi_ref[...]) + tn(gneg_ref[...], lo_ref[...])
    wide_ref[...] = wide.reshape(2, 64, 8, 512)
    sib_out[...] = wide_ref[other].astype(BF16)
    to_sib = remote(sib_out, sib_in, sib_send.at[2], sib_recv.at[2], sibling)
    to_sib.start()
    grad_ref[...] += degree * nn(gneg_ref[...], negs)
    to_sib.wait()
    rs_out[...] = (wide_ref[core] + sib_in[...].astype(F32)).astype(BF16)
    rs_in[chip] = rs_out[chip]
    spread(lambda to: rs_out.at[to], rs_in.at[chip], 2)

    loss = 0.5 * jnp.sum(loss_pos) + jnp.sum(loss_neg) * (1.0 / 1024)
    lane = lax.broadcasted_iota(jnp.int32, (8, 128), 1)
    total = jnp.where(
        lane == 0, loss, jnp.where(lane == 1, count.astype(F32) * 256.0, 0.0)
    )

    arrived(rs_in, 2)
    left(rs_out, 2)
    neg_total = jnp.sum(rs_in[...].astype(F32), axis=0)
    hi, lo = split(neg_total)
    row_at = lax.broadcasted_iota(jnp.int32, (512, 8), 0)
    lane_at = lax.broadcasted_iota(jnp.int32, (512, 8), 1)
    named = jnp.zeros((512, 8), jnp.int32)
    for j in range(8):
        named = jnp.where(lane_at == j, ids_ref[j], named)
    put = jnp.where(named == row_at, 1.0, 0.0).astype(BF16)
    pre = (grad_ref[...] + nn(put, hi) + nn(put, lo)).astype(BF16)
    pre_ref[...] = pre

    half = pl.ds(pl.multiple_of(core * 256, 256), 256)
    other_half = pl.ds(pl.multiple_of(other * 256, 256), 256)
    sends = []
    for r in range(3):
        x = feat_ref[...] if r == 0 else mean_ref[r - 1]
        part_ref[r] = tn(x, pre)
        c = remote(
            part_ref.at[r, other_half],
            wsib_ref.at[r],
            w_send.at[6, r],
            w_recv.at[6, r],
            sibling,
        )
        c.start()
        sends.append(c)
    t_out[0] = total
    c = remote(t_out.at[0], t_in.at[3, 0], t_send.at[3], t_recv.at[3], sibling)
    c.start()
    sends.append(c)
    for c in sends:
        c.wait()
    total = total + t_in[3, 0]
    for r in range(3):
        part_ref[r, half, :] += wsib_ref[r]

    def peers(axis):
        mine, stride = coords[axis], STRIDES[axis]
        found = []
        for s in range(1, 4):
            q = (mine + s) % 4
            found.append((q, me + (q - mine) * stride))
        return mine, found

    def settle(buf, sems, i, j):
        whole = buf.at[pl.ds(0, 3)]
        remote(whole, whole, sems[0].at[i, j], sems[1].at[i, j], sibling).wait()

    landing = (s1_ref, s2_ref, s3_ref)
    for stage in range(3):
        t_out[stage + 1] = total
        for r in range(3):
            mine, found = peers((r + stage) % 3)
            for q, to in found:
                if stage == 0:
                    start = pl.multiple_of(core * 256 + q * 64, 64)
                    src = part_ref.at[r, pl.ds(start, 64)]
                elif stage == 1:
                    src = a1_ref.at[r, pl.ds(pl.multiple_of(q * 16, 16), 16)]
                else:
                    src = a2_ref.at[r, :, pl.ds(pl.multiple_of(q * 128, 128), 128)]
                slot = (mine - q + 4) % 4 - 1
                remote(
                    src,
                    landing[stage].at[r, slot],
                    w_send.at[stage, r],
                    w_recv.at[stage, r],
                    to,
                ).start()
        mine, found = peers(stage)
        for q, to in found:
            slot = (mine - q + 4) % 4 - 1
            remote(
                t_out.at[stage + 1],
                t_in.at[stage, slot],
                t_send.at[stage],
                t_recv.at[stage],
                to,
            ).start()
        for r in range(3):
            mine = coords[(r + stage) % 3]
            settle(landing[stage].at[r], (w_send, w_recv), stage, r)
            got = landing[stage][r]
            got = got[0] + got[1] + got[2]
            if stage == 0:
                start = pl.multiple_of(core * 256 + mine * 64, 64)
                a1_ref[r] = part_ref[r, pl.ds(start, 64), :] + got
            elif stage == 1:
                rows = pl.ds(pl.multiple_of(mine * 16, 16), 16)
                a2_ref[r] = a1_ref[r, rows, :] + got
            else:
                lanes = pl.ds(pl.multiple_of(mine * 128, 128), 128)
                a3_ref[r] = a2_ref[r, :, lanes] + got
        whole = t_in.at[stage]
        remote(whole, whole, t_send.at[stage], t_recv.at[stage], sibling).wait()
        total = total + t_in[stage, 0] + t_in[stage, 1] + t_in[stage, 2]

    edges = total[:, 1:2]
    stat_ref[...] = total / edges
    inverse = jnp.sum(jnp.where(lane == 1, total, 0.0)) * 0.125
    for stage in (2, 1, 0):
        for r in range(3):
            q1, q2, q3 = (coords[(r + s) % 3] for s in range(3))
            if stage == 2:
                start = pl.multiple_of(core * 256 + q1 * 64 + q2 * 16, 16)
                spot = (pl.ds(start, 16), pl.ds(pl.multiple_of(q3 * 128, 128), 128))
                wout_ref[r, spot[0], spot[1]] = a3_ref[r] / inverse
            elif stage == 1:
                start = pl.multiple_of(core * 256 + q1 * 64 + q2 * 16, 16)
                spot = (pl.ds(start, 16), slice(None))
            else:
                start = pl.multiple_of(core * 256 + q1 * 64, 64)
                spot = (pl.ds(start, 64), slice(None))
            block = wout_ref.at[r, spot[0], spot[1]]
            mine, found = peers((r + stage) % 3)
            for q, to in found:
                remote(
                    block, block, w_send.at[3 + stage, r], w_recv.at[3 + stage, r], to
                ).start()
        for r in range(3):
            settle(landing[stage].at[r], (w_send, w_recv), 3 + stage, r)
    sends = []
    for r in range(3):
        block = wout_ref.at[r, half]
        c = remote(block, block, w_send.at[7, r], w_recv.at[7, r], sibling)
        c.start()
        sends.append(c)
    for c in sends:
        c.wait()


def on_device(features, weights, halo_send, nbr_index, tile_count, edge_ends, neg_ids):
    vmem = pl.BlockSpec(memory_space=pltpu.VMEM)
    smem = pl.BlockSpec(memory_space=pltpu.SMEM)
    dma = pltpu.SemaphoreType.DMA
    wout, stat, pre = pl.pallas_call(
        kernel,
        out_shape=(
            jax.ShapeDtypeStruct((3, 512, 512), F32),
            jax.ShapeDtypeStruct((8, 128), F32),
            jax.ShapeDtypeStruct((512, 512), BF16),
        ),
        in_specs=[smem, smem] + [vmem] * 5,
        out_specs=(vmem, vmem, vmem),
        scratch_shapes=[
            pltpu.VMEM((64, 8, 512), BF16),
            pltpu.VMEM((2, 64, 8, 512), BF16),
            pltpu.VMEM((2, 512, 1536), BF16),
            pltpu.VMEM((2, 512, 512), BF16),
            pltpu.VMEM((512, 512), BF16),
            pltpu.VMEM((512, 1024), BF16),
            pltpu.VMEM((512, 1024), BF16),
            pltpu.VMEM((512, 512), F32),
            pltpu.VMEM((512, 512), F32),
            pltpu.VMEM((512, 512), F32),
            pltpu.VMEM((512, 512), BF16),
            pltpu.VMEM((512, 512), BF16),
            pltpu.VMEM((8, 512), BF16),
            pltpu.VMEM((2, 64, 8, 512), BF16),
            pltpu.VMEM((512, 1024), F32),
            pltpu.VMEM((512, 1024), BF16),
            pltpu.VMEM((512, 512), F32),
            pltpu.VMEM((2, 64, 8, 512), F32),
            pltpu.VMEM((64, 8, 512), BF16),
            pltpu.VMEM((64, 8, 512), BF16),
            pltpu.VMEM((64, 8, 512), BF16),
            pltpu.VMEM((64, 8, 512), BF16),
            pltpu.VMEM((3, 512, 512), F32),
            pltpu.VMEM((3, 256, 512), F32),
            pltpu.VMEM((3, 3, 64, 512), F32),
            pltpu.VMEM((3, 3, 16, 512), F32),
            pltpu.VMEM((3, 3, 16, 128), F32),
            pltpu.VMEM((3, 64, 512), F32),
            pltpu.VMEM((3, 16, 512), F32),
            pltpu.VMEM((3, 16, 128), F32),
            pltpu.VMEM((4, 8, 128), F32),
            pltpu.VMEM((4, 3, 8, 128), F32),
            dma((3,)),
            dma((3,)),
            dma((3,)),
            dma((3,)),
            dma((8, 3)),
            dma((8, 3)),
            dma((4,)),
            dma((4,)),
        ],
        compiler_params=pltpu.CompilerParams(
            collective_id=0, has_side_effects=True, vmem_limit_bytes=60 * 1024 * 1024
        ),
    )(
        tile_count,
        neg_ids,
        features,
        weights,
        halo_send.reshape(1, 512),
        nbr_index.reshape(512, 16),
        edge_ends.reshape(16, 512),
    )
    return wout, stat[0, 0], pre


def solution(mesh):
    dom = ("dom",)
    in_specs = (
        P("dom", None),
        P(),
        P("dom", None, None),
        P("dom", None, None),
        P("dom"),
        P("dom", None, None),
        P("dom"),
    )
    return jax.shard_map(
        on_device,
        mesh=mesh,
        in_specs=in_specs,
        out_specs=(P(), P(), P("dom", None)),
        check_vma=False,
    )
```

time: 505 us -> 111 us (0.22); the launches traced: 497 us -> 110 us
  starting transfers between devices: 171 us -> 0 us
  local copies, waits for them, and re-layouts: 142 us -> 10.3 us
  Pallas kernels: 0 us -> 98.6 us
  blocking collectives: 86.8 us -> 0 us
  other arithmetic: 35.1 us -> 0 us
  waiting for transfers between devices: 33 us -> 0 us
  matrix products: 19.4 us -> 0 us
  between operations: 6.44 us -> 1.29 us
    all_to_all x3 -> x0, starting transfers between devices: 164 us -> none  [the longest x1 148 us: sum_by_axis(): return jnp.sum(lax.all_to_all(own, far, 0, 0, tiled=True), axis=0)]
    pallas_call x0 -> x1, Pallas kernels: none -> 98.6 us  [on_device(): pl.pallas_call(kernel, out_shape=(jax.ShapeDtypeStruct((3, 512, 512), F32...]
    all_to_all x6 -> x0, blocking collectives: 86.8 us -> none  [the longest x3 43.3 us: sent_to_all(): return lax.all_to_all(copies, axis, split_axis=0, concat_axis=0, tiled=True)]
    gather x23 -> x0, local copies, waits for them, and re-layouts: 66.2 us -> none  [the longest x16 52.8 us: neighbour_mean(): lookup[neighbours[:, column]].astype(jnp.float32)]
    all_to_all x3 -> x0, waiting for transfers between devices: 32.4 us -> none  [the longest x1 18 us: sum_by_axis(): return jnp.sum(lax.all_to_all(own, far, 0, 0, tiled=True), axis=0)]
    concatenate x2 -> x0, local copies, waits for them, and re-layouts: 26.7 us -> none  [the longest x1 25.6 us: together(): jnp.concatenate([a.reshape(-1) for a in arrays])]
    dot_general x12 -> x0, matrix products: 19.4 us -> none  [the longest x2 7.55 us: score_tile(): lax.dot_general(grad_negative, source, (((0,), (0,)), ((), ())), preferre...]
    another operation x5 -> x0, local copies, waits for them, and re-layouts: 16.6 us -> none  [the longest x1 6.69 us: split_up(): x.reshape(*dims[:dim], devices, dims[dim] // devices, *dims[dim + 1:])]
  transfers between devices with their start and end apart: 7 -> 0, of which waited for: 4 -> 0; matrix products, arithmetic and copies ran while one was open for 6% -> 0% of each run, Pallas kernels for 0% -> 0%
where the time goes in v1:
time: 111 us; the launch traced here: 110 us
  Pallas kernels  98.6 us (89%)
  local copies, waits for them, and re-layouts  10.3 us (9%)
  between operations  1.29 us (1%)
    pallas_call x1, Pallas kernels, on_device(): pl.pallas_call(kernel, out_shape=(jax.ShapeDtypeStruct((3, 512, 512), F32...  98.6 us
    unnamed x6, local copies, waits for them, and re-layouts  6.88 us

profile of v1, /device:TPU:1, one launch (start us, length us, event | category | flops | bytes accessed | tf_op | source)
XLA Modules:
  0.0 110.2 jit_solution(11329028932967605212)
XLA Ops:
  1.3 1.4 %copy.14 = s32[2,8,2,256]{3,1,2,0:T(8,128)} copy(s32[2,8,2,256]{3,2,1,0:T(2,128)} %bitcast.6) | data formatting | bytes 65536
  2.7 0.8 copy.12
  3.4 0.7 reshape.15.halo_ref
  4.1 1.6 %copy.13.nbr_ref = s32[512,16]{1,0:T(8,128)} copy(s32[512,16]{0,1:T(8,128)} %bitcast.5) | data formatting | bytes 65536 | tf_op jit(solution)/shard_map/reshape | solution.py:475
  5.7 98.6 %shard_map.94 = (f32[3,512,512]{2,1,0:T(8,128)}, f32[8,128]{1,0:T(8,128)}, bf16[512,512]{1,0:T(8,128)(2,1)}) custom-call(s32[1]{0:T(128)S(6)} %copy.17.count_ref, s32[8]{0:T(128)} %ids_ref.1, bf16[512,512]{1,0:T(8,128)(2,1)} %feat_ref.1, bf16[3,512,512]{2,1,0:T(8,128)(2,1)} %wts_ref.1, s32[1,512]{1,0:T(1,128)} %reshape.15.halo_ref, s32[512,16]{1,0:T(8,128)} %copy.13.nbr_ref, ...), custom_call_target="tpu_custom_call" | custom-call | tf_op jit(solution)/shard_map/pallas_call | solution.py:415
  104.3 1.2 %slice.3 = f32[1,1]{1,0:T(1,128)} slice(f32[8,128]{1,0:T(8,128)} %get-tuple-element.7), slice={[0:1], [0:1]} | slice | bytes 8 | tf_op jit(solution)/shard_map/slice | solution.py:478
  105.5 0.0 copy-start
  105.5 3.9 %copy.18 = f32[3,512,512]{2,1,0:T(8,128)} copy(f32[3,512,512]{2,1,0:T(8,128)} %get-tuple-element.12) | data formatting | bytes 6291456
  109.4 0.0 copy-done
  109.4 0.8 copy.19
Async XLA Ops:
  105.5 3.9 %copy-start = (bf16[512,512]{1,0:T(8,128)(2,1)S(1)}, bf16[512,512]{1,0:T(8,128)(2,1)}, u32[]{:S(2)}) copy-start(bf16[512,512]{1,0:T(8,128)(2,1)} %get-tuple-element.14) | copy-start | bytes 1572868
